TPU v7x, 512 devices: a whole 4x4x16 slice. The times are simulated.
512 devices in a mesh: cells: 32 (over x, y, core), vocab: 16 (over z).
Axes of the slice: x: 4, y: 4, z: 16, core: 2. Of those that a mesh axis runs over, the one named last changes fastest.
Arguments:
- clean_resid: float32 [32, 2048], P('cells'), may hold values from -130 to 130
- path_delta: bfloat16 [32, 4, 16, 2048], P('cells'), may hold values from -6 to 6
- layer_index: int32 [4064], P('cells'), may hold values from 0 to 3
- pos_index: int32 [4064], P('cells'), may hold values from 0 to 15
- answer_ids: int32 [32], P('cells'), may hold values from 0 to 51199
- norm_gain: float32 [2048], replicated, may hold values from 0.1 to 1.9
- unembed: bfloat16 [2048, 51200], P('cells', 'vocab'), may hold values from -1.5 to 1.5
Outputs:
- divergence: float32 [4064], P('cells')
- answer_logprob: float32 [4064], P('cells')
- total_kl: float32 [], replicated
All inputs are finite; a program needn't handle non-finite values.
Results may differ from a plain program's by a relative error of at most 0.0091.
Values may be sent and summed in bfloat16 or wider, within the bound.
No kernel may reach another device: no remote copies, remote signals or barrier semaphores. Data moves between devices by JAX's collectives and lax.ppermute only.
A program may use at most 64 MiB of HBM per device.

v0:
```python
import jax
import jax.numpy as jnp
from jax import lax
from jax.sharding import PartitionSpec as P


def sent_to_all(value, axis):
    length = lax.axis_size(axis)
    return lax.all_to_all(
        jnp.broadcast_to(value[None], (length, *value.shape)), axis, 0, 0, tiled=True
    )


def collected_together(value, axis):
    leaves = jax.tree.leaves(value)
    sequence = sorted(range(len(leaves)), key=lambda k: -leaves[k].size)
    width = (1, *leaves[sequence[0]].shape)[-1]
    lines = [
        jnp.pad(leaves[k].reshape(-1), (0, -leaves[k].size % width)).reshape(-1, width)
        for k in sequence
    ]
    both, at, found = (sent_to_all(jnp.concatenate(lines), axis), 0, {})
    for k, line in zip(sequence, lines):
        slab = both[:, at : at + len(line)].reshape(len(both), -1)
        found[k] = slab[:, : leaves[k].size].reshape(-1, *leaves[k].shape)
        at += len(line)
    numbers = iter(range(len(leaves)))
    return jax.tree.map(lambda _: found[next(numbers)], value)


def folded_in_pairs(pieces, combine):
    while len(jax.tree.leaves(pieces)[0]) > 1:
        pieces = jax.vmap(combine)(
            *(jax.tree.map(lambda part: part[side::2], pieces) for side in (0, 1))
        )
    return jax.tree.map(lambda part: part[0], pieces)


def merged_2(value, axis, combine):
    pieces = collected_together(value, axis)
    return folded_in_pairs(pieces, combine)


def of_everyone(value, axis):
    everything = sent_to_all(value, axis)
    return jnp.sum(everything, axis=0)


def normalize_rows(values, norm_gain):
    mean_square = jnp.mean(values * values, axis=-1, keepdims=True)
    return (values * lax.rsqrt(mean_square + 1e-06) * norm_gain).astype(jnp.bfloat16)


def local_partials(clean_logits, patched_logits, answer_mask, max_clean, max_patch):
    clean_exp = jnp.exp(clean_logits - max_clean[:, None])
    sum_clean = jnp.sum(clean_exp, axis=-1)
    cross_term = jnp.sum(
        clean_exp[:, None, :] * (clean_logits[:, None, :] - patched_logits), axis=-1
    )
    sum_patch = jnp.sum(jnp.exp(patched_logits - max_patch[..., None]), axis=-1)
    answer_sum = jnp.sum(jnp.where(answer_mask[:, None, :], patched_logits, 0.0), axis=-1)
    return (sum_clean, cross_term, sum_patch, answer_sum)


def combine_stats(earlier, later):
    max_one, sum_one, cross_one, patch_one, spat_one, answer_one = earlier
    max_two, sum_two, cross_two, patch_two, spat_two, answer_two = later
    max_clean = jnp.maximum(max_one, max_two)
    factor_one = jnp.exp(max_one - max_clean)
    factor_two = jnp.exp(max_two - max_clean)
    max_patch = jnp.maximum(patch_one, patch_two)
    pfactor_one = jnp.exp(patch_one - max_patch)
    pfactor_two = jnp.exp(patch_two - max_patch)
    return (
        max_clean,
        sum_one * factor_one + sum_two * factor_two,
        cross_one * factor_one[:, None] + cross_two * factor_two[:, None],
        max_patch,
        spat_one * pfactor_one + spat_two * pfactor_two,
        answer_one + answer_two,
    )


def finish_stats(max_clean, sum_clean, cross_term, max_patch, sum_patch, answer_sum):
    clean_lse = max_clean + jnp.log(sum_clean)
    patched_lse = max_patch + jnp.log(sum_patch)
    divergence = cross_term / sum_clean[:, None] - clean_lse[:, None] + patched_lse
    return (divergence, answer_sum - patched_lse)


def reduce_vocab(clean_logits, patched_logits, answer_mask):
    max_clean = jnp.max(clean_logits, axis=-1)
    max_patch = jnp.max(patched_logits, axis=-1)
    sum_clean, cross_term, sum_patch, answer_sum = local_partials(
        clean_logits, patched_logits, answer_mask, max_clean, max_patch
    )
    merged = merged_2(
        (max_clean, sum_clean, cross_term, max_patch, sum_patch, answer_sum), "vocab", combine_stats
    )
    return finish_stats(*merged)


def on_device(clean_resid, path_delta, layer_index, pos_index, answer_ids, norm_gain, unembed):
    position_count = path_delta.shape[2]
    table_rows = path_delta.shape[1] * position_count
    feature_count = clean_resid.shape[1]
    flat_index = layer_index * position_count + pos_index
    shard_width = unembed.shape[1]
    vocab_start = lax.axis_index("vocab") * shard_width
    delta_table = path_delta.reshape(table_rows, feature_count)
    picker = (flat_index[:, None] == jnp.arange(table_rows, dtype=jnp.int32)[None, :]).astype(
        jnp.bfloat16
    )
    patched_resid = clean_resid + jnp.dot(picker, delta_table, preferred_element_type=jnp.float32)
    stacked = jnp.concatenate(
        [normalize_rows(clean_resid, norm_gain), normalize_rows(patched_resid, norm_gain)], axis=0
    )
    logits = jnp.dot(
        stacked,
        lax.all_gather(unembed, "cells", axis=0, tiled=True),
        preferred_element_type=jnp.float32,
    )
    columns = vocab_start + jnp.arange(shard_width, dtype=jnp.int32)
    answer_mask = columns[None, :] == answer_ids[:, None]
    divergence, answer_logprob = reduce_vocab(logits[:1], logits[1:][None], answer_mask)
    divergence = divergence[0]
    answer_logprob = answer_logprob[0]
    total_kl = of_everyone(jnp.sum(divergence), "cells")
    return (divergence, answer_logprob, total_kl)


def solution(mesh):
    in_specs = (
        P("cells", None),
        P("cells", None, None, None),
        P("cells"),
        P("cells"),
        P("cells"),
        P(),
        P("cells", "vocab"),
    )
    out_specs = (P("cells"), P("cells"), P())
    return jax.shard_map(
        on_device, mesh=mesh, in_specs=in_specs, out_specs=out_specs, check_vma=False
    )
```

profile of v0, /device:TPU:1, one launch (start us, length us, event | category | flops | bytes accessed | tf_op | source)
XLA Modules:
  0.0 160.9 jit_solution(15475572089582252857)
XLA Ops:
  7.2 0.0 copy-start
  7.2 0.0 copy-start.1
  7.2 0.0 all-gather.2.cloned.1.call-start
  7.2 0.7 all-gather.2.cloned.1.call-update
  7.9 1.3 multiply_reduce_fusion.2
  10.6 0.7 multiply_add_fusion.9
  11.3 0.0 copy-done
  11.3 1.1 multiply_reduce_fusion.1
  12.5 0.0 copy-done.1
  12.5 0.2 multiply_convert_fusion
  12.7 83.6 %all-gather.2.cloned.1.call-done = bf16[2048,3200]{1,0:T(8,128)(2,1)} async-done(((bf16[64,3200]{1,0:T(8,128)(2,1)}), bf16[2048,3200]{1,0:T(8,128)(2,1)}) %all-gather.2.cloned.1.call-update) | async-done | bytes 13107216 | tf_op jit(solution)/shard_map/all_gather | solution.py:120
  96.2 6.7 %fusion = f32[128,3200]{1,0:T(8,128)S(1)} fusion(bf16[2048,3200]{1,0:T(8,128)(2,1)} %all-gather.2.cloned.1.call-done, bf16[127,2048]{1,0:T(8,128)(2,1)S(1)} %multiply_convert_fusion, bf16[1,2048]{1,0:T(2,128)(2,1)S(1)} %multiply_convert_fusion.1), kind=kOutput, calls=%fused_computation.7 | convolution fusion | flops 1678770176 | bytes 15269888 | tf_op jit(solution)/shard_map/dot_general | solution.py:118
  102.9 0.6 slice_reduce_fusion.2
  103.6 1.3 fusion.17
  104.9 0.6 select_reduce_fusion
  105.5 0.5 exponential_reduce_fusion
  105.9 1.3 pad_bitcast_fusion
  107.3 23.4 %all_to_all.11 = f32[16,6,127]{2,1,0:T(8,128)S(1)} all-to-all(f32[16,6,127]{2,1,0:T(8,128)S(1)} %broadcast_in_dim.17), channel_id=1, replica_groups=mesh['cells'=32,'vocab'=16] {'vocab'}, dimensions={0} | all-to-all | bytes 97536 | tf_op jit(solution)/shard_map/all_to_all | solution.py:9
  131.0 0.2 fusion.7
  131.1 0.2 fusion.5
  131.3 0.2 fusion.14
  131.5 0.5 fusion.22
  134.6 0.5 fusion.21
  136.6 0.1 multiply_add_fusion.2
  136.7 0.1 multiply_add_fusion.5
  136.8 0.1 multiply_add_fusion.8
  136.8 1.1 fusion.19
  138.0 1.2 broadcast_in_dim.22
  139.1 7.3 %all-to-all-start.1 = ((f32[32,1,1]{2,1,0:T(1,128)}), f32[32,1,1]{2,1,0:T(1,128)S(1)}, u32[]{:S(2)}, u32[]{:S(2)}) async-start(f32[32,1,1]{2,1,0:T(1,128)} %broadcast_in_dim.22), calls=%async_computation.1 | async-start | bytes 32768 | tf_op jit(solution)/shard_map/all_to_all | solution.py:9
  146.5 0.5 fusion.13
  147.0 6.4 %all-to-all-done.1 = f32[32,1,1]{2,1,0:T(1,128)S(1)} async-done(((f32[32,1,1]{2,1,0:T(1,128)}), f32[32,1,1]{2,1,0:T(1,128)S(1)}, u32[]{:S(2)}, u32[]{:S(2)}) %all-to-all-start.1) | async-done | bytes 160 | tf_op jit(solution)/shard_map/all_to_all | solution.py:9
  153.4 0.6 reduce_sum.91
  (29 shorter events, 0.4 us)
Async XLA Ops:
  7.2 4.1 %copy-start = (bf16[1,4,16,2048]{3,2,1,0:T(8,128)(2,1)S(1)}, bf16[1,4,16,2048]{3,2,1,0:T(8,128)(2,1)}, u32[]{:S(2)}) copy-start(bf16[1,4,16,2048]{3,2,1,0:T(8,128)(2,1)} %param.8) | copy-start | bytes 786436
  7.2 5.3 %copy-start.1 = (f32[1,2048]{1,0:T(1,128)S(1)}, f32[1,2048]{1,0:T(1,128)}, u32[]{:S(2)}) copy-start(f32[1,2048]{1,0:T(1,128)} %param.7) | copy-start | bytes 24580
  7.2 5.3 %copy-start.2 = (f32[2048]{0:T(1024)S(1)}, f32[2048]{0:T(1024)}, u32[]{:S(2)}) copy-start(f32[2048]{0:T(1024)} %param.12) | copy-start | bytes 24580
  7.2 89.0 %all-gather.2.cloned.1.call-start = ((), (), s32[]{:S(2)}) async-start(), calls=%async_computation.2 | async-start | bytes 13516800 | tf_op jit(solution)/shard_map/all_gather | solution.py:120
  139.1 14.3 %all-to-all-start.1 = ((f32[32,1,1]{2,1,0:T(1,128)}), f32[32,1,1]{2,1,0:T(1,128)S(1)}, u32[]{:S(2)}, u32[]{:S(2)}) async-start(f32[32,1,1]{2,1,0:T(1,128)} %broadcast_in_dim.22), calls=%async_computation.1 | async-start | bytes 32768 | tf_op jit(solution)/shard_map/all_to_all | solution.py:9
Sparse Core Ops, SparseCore 0:
  11.1 85.0 all-gather.1
where the time goes:
time: 161 us
  waiting for transfers between devices  90.7 us (56%)
  blocking collectives  23.4 us (15%)
  between operations  19.6 us (12%)
  other arithmetic  8.24 us (5%)
  matrix products  7.84 us (5%)
  starting transfers between devices  7.34 us (5%)
  local copies, waits for them, and re-layouts  3.83 us (2%)
    all_gather x1, waiting for transfers between devices, on_device(): lax.all_gather(unembed, 'cells', axis=0, tiled=True)  83.6 us
    all_to_all x1, blocking collectives, sent_to_all(): lax.all_to_all(jnp.broadcast_to(value[None], (length, *value.shape)), axi...  23.4 us
    all_to_all x1, starting transfers between devices, sent_to_all(): lax.all_to_all(jnp.broadcast_to(value[None], (length, *value.shape)), axi...  7.3 us
    dot_general x1, matrix products, on_device(): jnp.dot(stacked, lax.all_gather(unembed, 'cells', axis=0, tiled=True), pr...  6.69 us
    all_to_all x1, waiting for transfers between devices, sent_to_all(): lax.all_to_all(jnp.broadcast_to(value[None], (length, *value.shape)), axi...  6.42 us
  transfers between devices with their start and end apart: 2, of which 2 were waited for; matrix products, arithmetic and copies ran while one was open for 2% of the time, Pallas kernels for 0%

commit v1 on v0

--- a/solution.py
+++ b/solution.py
@@ -2,6 +2,11 @@
 import jax.numpy as jnp
 from jax import lax
 from jax.sharding import PartitionSpec as P
+
+
+def tiled_gather(value, axis, dim):
+    copies = jnp.concatenate([value] * lax.axis_size(axis), axis=dim)
+    return lax.all_to_all(copies, axis, dim, dim, tiled=True)
 
 
 def sent_to_all(value, axis):
@@ -115,11 +120,7 @@
     stacked = jnp.concatenate(
         [normalize_rows(clean_resid, norm_gain), normalize_rows(patched_resid, norm_gain)], axis=0
     )
-    logits = jnp.dot(
-        stacked,
-        lax.all_gather(unembed, "cells", axis=0, tiled=True),
-        preferred_element_type=jnp.float32,
-    )
+    logits = jnp.dot(stacked, tiled_gather(unembed, "cells", 0), preferred_element_type=jnp.float32)
     columns = vocab_start + jnp.arange(shard_width, dtype=jnp.int32)
     answer_mask = columns[None, :] == answer_ids[:, None]
     divergence, answer_logprob = reduce_vocab(logits[:1], logits[1:][None], answer_mask)

time: 161 us -> 298 us (1.85)
  waiting for transfers between devices: 90.7 us -> 184 us
  starting transfers between devices: 7.34 us -> 40.1 us
  local copies, waits for them, and re-layouts: 3.83 us -> 25.8 us
  between operations: 19.6 us -> 6.34 us
  blocking collectives: 23.4 us -> 26.8 us
    all_to_all x0 -> x1, waiting for transfers between devices: none -> 178 us  [tiled_gather(): return lax.all_to_all(copies, axis, dim, dim, tiled=True)]
    all_gather x1 -> x0, waiting for transfers between devices: 83.6 us -> none  [on_device(): lax.all_gather(unembed, 'cells', axis=0, tiled=True)]
    unnamed x6 -> x45, local copies, waits for them, and re-layouts: 0.02 us -> 22 us
    all_to_all x1, starting transfers between devices: 7.3 us -> 28.5 us  [sent_to_all(): lax.all_to_all(jnp.broadcast_to(value[None], (length, *value.shape)), axi...]
    all_to_all x0 -> x1, starting transfers between devices: none -> 11.6 us  [tiled_gather(): return lax.all_to_all(copies, axis, dim, dim, tiled=True)]
    all_to_all x1, blocking collectives: 23.4 us -> 26.8 us  [sent_to_all(): lax.all_to_all(jnp.broadcast_to(value[None], (length, *value.shape)), axi...]
  transfers between devices with their start and end apart: 2 -> 2, of which waited for: 2 -> 2; matrix products, arithmetic and copies ran while one was open for 2% -> 1% of each run, Pallas kernels for 0% -> 0%
where the time goes in v1:
time: 298 us; the launch traced here: 297 us
  waiting for transfers between devices  184 us (62%)
  starting transfers between devices  40.1 us (13%)
  blocking collectives  26.8 us (9%)
  local copies, waits for them, and re-layouts  25.8 us (9%)
  matrix products  7.12 us (2%)
  other arithmetic  6.87 us (2%)
  between operations  6.34 us (2%)
    all_to_all x1, waiting for transfers between devices, tiled_gather(): return lax.all_to_all(copies, axis, dim, dim, tiled=True)  178 us
    all_to_all x1, starting transfers between devices, sent_to_all(): lax.all_to_all(jnp.broadcast_to(value[None], (length, *value.shape)), axi...  28.5 us
    all_to_all x1, blocking collectives, sent_to_all(): lax.all_to_all(jnp.broadcast_to(value[None], (length, *value.shape)), axi...  26.8 us
    unnamed x45, local copies, waits for them, and re-layouts  22 us
    all_to_all x1, starting transfers between devices, tiled_gather(): return lax.all_to_all(copies, axis, dim, dim, tiled=True)  11.6 us
    dot_general x1, matrix products, on_device(): jnp.dot(stacked, tiled_gather(unembed, 'cells', 0), preferred_element_typ...  6.69 us
    all_to_all x1, waiting for transfers between devices, sent_to_all(): lax.all_to_all(jnp.broadcast_to(value[None], (length, *value.shape)), axi...  6.46 us
  transfers between devices with their start and end apart: 2, of which 2 were waited for; matrix products, arithmetic and copies ran while one was open for 1% of the time, Pallas kernels for 0%

profile of v1, /device:TPU:1, one launch (start us, length us, event | category | flops | bytes accessed | tf_op | source)
XLA Modules:
  0.0 297.3 jit_solution(8863078326007066246)
XLA Ops:
  0.7 1.1 constant_dynamic-update-slice_fusion.31
  1.8 1.0 constant_dynamic-update-slice_fusion.30
  2.8 1.0 constant_dynamic-update-slice_fusion.29
  3.8 1.0 constant_dynamic-update-slice_fusion.28
  4.9 1.0 constant_dynamic-update-slice_fusion.27
  5.9 1.0 constant_dynamic-update-slice_fusion.26
  7.0 1.0 constant_dynamic-update-slice_fusion.25
  8.0 1.0 constant_dynamic-update-slice_fusion.24
  9.0 1.0 constant_dynamic-update-slice_fusion.23
  10.1 1.0 constant_dynamic-update-slice_fusion.22
  11.1 1.0 constant_dynamic-update-slice_fusion.21
  12.2 1.0 constant_dynamic-update-slice_fusion.20
  13.2 1.0 constant_dynamic-update-slice_fusion.19
  14.2 1.0 constant_dynamic-update-slice_fusion.18
  15.3 1.0 constant_dynamic-update-slice_fusion.17
  16.3 1.0 constant_dynamic-update-slice_fusion.16
  18.1 4.7 %copy-done.2 = bf16[2048,3200]{1,0:T(8,128)(2,1)} copy-done((bf16[2048,3200]{1,0:T(8,128)(2,1)}, bf16[2048,3200]{1,0:T(8,128)(2,1)S(1)}, u32[]{:S(2)}) %copy-start.2) | copy-done | bytes 13107224
  22.8 11.6 %all-to-all-start = ((bf16[32,64,3200]{2,1,0:T(8,128)(2,1)}), bf16[32,64,3200]{2,1,0:T(8,128)(2,1)}, u32[]{:S(2)}, u32[]{:S(2)}) async-start(bf16[32,64,3200]{2,1,0:T(8,128)(2,1)} %bitcast.33), calls=%async_computation | async-start | bytes 26214400 | tf_op jit(solution)/shard_map/all_to_all | solution.py:9
  34.4 0.6 multiply_reduce_fusion.2
  37.1 177.8 %all-to-all-done = bf16[32,64,3200]{2,1,0:T(8,128)(2,1)} async-done(((bf16[32,64,3200]{2,1,0:T(8,128)(2,1)}), bf16[32,64,3200]{2,1,0:T(8,128)(2,1)}, u32[]{:S(2)}, u32[]{:S(2)}) %all-to-all-start) | async-done | bytes 13107232 | tf_op jit(solution)/shard_map/all_to_all | solution.py:9
  214.9 6.7 %fusion = f32[128,3200]{1,0:T(8,128)S(1)} fusion(bf16[2048,3200]{1,0:T(8,128)(2,1)} %bitcast.4, bf16[127,2048]{1,0:T(8,128)(2,1)S(1)} %multiply_convert_fusion, bf16[1,2048]{1,0:T(2,128)(2,1)S(1)} %multiply_convert_fusion.1), kind=kOutput, calls=%fused_computation.7 | convolution fusion | flops 1678770176 | bytes 15269888 | tf_op jit(solution)/shard_map/dot_general | solution.py:123
  221.6 0.6 slice_reduce_fusion.2
  222.2 1.3 fusion.17
  223.5 0.6 select_reduce_fusion
  224.5 1.3 pad_bitcast_fusion
  225.9 26.8 %all_to_all.23 = f32[16,6,127]{2,1,0:T(8,128)S(1)} all-to-all(f32[16,6,127]{2,1,0:T(8,128)S(1)} %broadcast_in_dim.17), channel_id=1, replica_groups=mesh['cells'=32,'vocab'=16] {'vocab'}, dimensions={0} | all-to-all | bytes 97536 | tf_op jit(solution)/shard_map/all_to_all | solution.py:14
  253.0 0.5 fusion.22
  258.9 1.1 fusion.19
  260.0 1.2 broadcast_in_dim.22
  261.2 28.5 %all-to-all-start.2 = ((f32[32,1,1]{2,1,0:T(1,128)}), f32[32,1,1]{2,1,0:T(1,128)S(1)}, u32[]{:S(2)}, u32[]{:S(2)}) async-start(f32[32,1,1]{2,1,0:T(1,128)} %broadcast_in_dim.22), calls=%async_computation.2 | async-start | bytes 32768 | tf_op jit(solution)/shard_map/all_to_all | solution.py:14
  290.2 6.5 %all-to-all-done.2 = f32[32,1,1]{2,1,0:T(1,128)S(1)} async-done(((f32[32,1,1]{2,1,0:T(1,128)}), f32[32,1,1]{2,1,0:T(1,128)S(1)}, u32[]{:S(2)}, u32[]{:S(2)}) %all-to-all-start.2) | async-done | bytes 160 | tf_op jit(solution)/shard_map/all_to_all | solution.py:14
  296.6 0.6 reduce_sum.91
  (68 shorter events, 3.8 us)
Async XLA Ops:
  0.6 35.8 %copy-start = (bf16[1,4,16,2048]{3,2,1,0:T(8,128)(2,1)S(1)}, bf16[1,4,16,2048]{3,2,1,0:T(8,128)(2,1)}, u32[]{:S(2)}) copy-start(bf16[1,4,16,2048]{3,2,1,0:T(8,128)(2,1)} %param.8) | copy-start | bytes 786436
  0.6 16.7 %copy-start.1 = (bf16[64,3200]{1,0:T(8,128)(2,1)S(1)}, bf16[64,3200]{1,0:T(8,128)(2,1)}, u32[]{:S(2)}) copy-start(bf16[64,3200]{1,0:T(8,128)(2,1)} %param.13) | copy-start | bytes 1228804
  18.0 4.7 %copy-start.2 = (bf16[2048,3200]{1,0:T(8,128)(2,1)}, bf16[2048,3200]{1,0:T(8,128)(2,1)S(1)}, u32[]{:S(2)}) copy-start(bf16[2048,3200]{1,0:T(8,128)(2,1)S(1)} %constant_dynamic-update-slice_fusion) | copy-start | bytes 39321604
  22.8 11.6 %copy-start.3 = (f32[1,2048]{1,0:T(1,128)S(1)}, f32[1,2048]{1,0:T(1,128)}, u32[]{:S(2)}) copy-start(f32[1,2048]{1,0:T(1,128)} %param.7) | copy-start | bytes 24580
  22.8 13.6 %copy-start.5 = (s32[127]{0:T(128)S(1)}, s32[127]{0:T(128)}, u32[]{:S(2)}) copy-start(s32[127]{0:T(128)} %param.10) | copy-start | bytes 1528
  22.8 13.6 %copy-start.6 = (s32[127]{0:T(128)S(1)}, s32[127]{0:T(128)}, u32[]{:S(2)}) copy-start(s32[127]{0:T(128)} %param.9) | copy-start | bytes 1528
  22.8 14.1 %copy-start.4 = (f32[2048]{0:T(1024)S(1)}, f32[2048]{0:T(1024)}, u32[]{:S(2)}) copy-start(f32[2048]{0:T(1024)} %param.12) | copy-start | bytes 24580
  22.8 192.1 %all-to-all-start = ((bf16[32,64,3200]{2,1,0:T(8,128)(2,1)}), bf16[32,64,3200]{2,1,0:T(8,128)(2,1)}, u32[]{:S(2)}, u32[]{:S(2)}) async-start(bf16[32,64,3200]{2,1,0:T(8,128)(2,1)} %bitcast.33), calls=%async_computation | async-start | bytes 26214400 | tf_op jit(solution)/shard_map/all_to_all | solution.py:9
  261.2 35.5 %all-to-all-start.2 = ((f32[32,1,1]{2,1,0:T(1,128)}), f32[32,1,1]{2,1,0:T(1,128)S(1)}, u32[]{:S(2)}, u32[]{:S(2)}) async-start(f32[32,1,1]{2,1,0:T(1,128)} %broadcast_in_dim.22), calls=%async_computation.2 | async-start | bytes 32768 | tf_op jit(solution)/shard_map/all_to_all | solution.py:14
